TPU v7x, 32 devices: a whole 2x2x4 slice. The times are simulated.
32 devices in a mesh: grp: 2 (over x), slab: 16 (over z, y, core).
Axes of the slice: x: 2, y: 2, z: 4, core: 2. Of those that a mesh axis runs over, the one named last changes fastest.
Arguments:
- volume: bfloat16 [64, 1024, 1024], P(('grp', 'slab')), parts along dimension 0, may hold values from -60 to 60
- plane_shift: int32 [4, 32], P('grp', 'slab'), parts along dimension 0, may hold values from -64 to 64
- plane_weight: float32 [4, 32], P('grp', 'slab'), parts along dimension 0, may hold values from 0 to 1
- column_left: int32 [4, 1024], P('grp'), parts along dimension 0, may hold values from 0 to 1022
- column_weight: float32 [4, 1024], P('grp'), parts along dimension 0, may hold values from 0 to 1
- window_center: int32 [4, 2], P('grp'), parts along dimension 0, may hold values from -200 to 199
- tilt_owner: int32 [32], P('grp'), parts along dimension 0, may hold values from 0 to 15, each once
- reference_band: float32 [32, 2, 128, 128], P(('grp', 'slab')), parts along dimension 0, may hold values from -6 to 6
Outputs:
- correlation: float32 [4, 16, 128], P('grp', 'slab'), parts along dimension 0
- peaks: float32 [4], P('grp'), parts along dimension 0
There are 2 independent parts, one for each index of `grp`. A program takes and returns all parts, laid end to end along the dimension named above; each array names one. Nothing has to cross between parts.
Inputs may be any that keep to these rules, and one draw needn't show every extreme that they name: `tilt_owner`: the first 2 entries name the owners of the tilts, one slab index each.
All inputs are finite; a program needn't handle non-finite values.
Results may differ from a plain program's by a relative error of at most 0.0003.
Values sent between devices are 32-bit elements; how exact they have to be, the bound alone decides.
A program may use at most 128 MiB of HBM per device.

v0:
```python
import math
import jax
import jax.numpy as jnp
from jax import lax
from jax.sharding import PartitionSpec as P

Y = 1024
X = 1024
BAND = 128
WIN_COLS = 128
TILTS = 2
WIN_ROWS_DEV = 1


def from_root(value, axis, source):
    kept = jnp.where(lax.axis_index(axis) == source, value, 0).astype(value.dtype)
    return lax.psum(kept, axis)


def phase_pair(left_ints, right_ints, length):
    product = left_ints[:, None] * right_ints[None, :] % length
    angle = product.astype(jnp.float32) * (2.0 * math.pi / length)
    return (jnp.cos(angle), jnp.sin(angle))


def matmul(first, second):
    return jnp.dot(
        first, second, precision=lax.Precision.HIGHEST, preferred_element_type=jnp.float32
    )


def reproject(volume, shifts, weights, left_cols, right_share, row_count):
    grid_width = volume.shape[2]
    margin = grid_width // 16 + 1
    padded_all = jnp.pad(volume, ((0, 0), (0, 0), (margin, margin)))
    summed = jnp.zeros((row_count, grid_width), jnp.float32)
    for plane_no in range(volume.shape[0]):
        padded = padded_all[plane_no]
        near_cells = lax.dynamic_slice_in_dim(
            padded, margin - shifts[plane_no], grid_width, 1
        ).astype(jnp.float32)
        far_cells = lax.dynamic_slice_in_dim(
            padded, margin - shifts[plane_no] - 1, grid_width, 1
        ).astype(jnp.float32)
        summed = summed + (1.0 - weights[plane_no]) * near_cells + weights[plane_no] * far_cells
    left_values = jnp.take(summed, left_cols, axis=1)
    right_values = jnp.take(summed, left_cols + 1, axis=1)
    return (1.0 - right_share) * left_values + right_share * right_values


def band_part(projected):
    row_count, grid_width = projected.shape
    freq_cols = jnp.arange(BAND, dtype=jnp.int32)
    freq_rows = freq_cols - BAND // 2
    col_cos, col_sin = phase_pair(jnp.arange(grid_width, dtype=jnp.int32), freq_cols, grid_width)
    real_half = matmul(projected, col_cos)
    imag_half = -matmul(projected, col_sin)
    row_ids = jnp.arange(row_count, dtype=jnp.int32)
    row_cos, row_sin = phase_pair(freq_rows, row_ids, Y)
    spec_real = matmul(row_cos, real_half) + matmul(row_sin, imag_half)
    spec_imag = matmul(row_cos, imag_half) - matmul(row_sin, real_half)
    return jnp.stack([spec_real, spec_imag])


def correlate(spectrum, owned, center, row_ids, total_rows):
    spec_real, spec_imag = (spectrum[0], spectrum[1])
    ref_real, ref_imag = (owned[0], owned[1])
    cross_real = spec_real * ref_real + spec_imag * ref_imag
    cross_imag = spec_imag * ref_real - spec_real * ref_imag
    energy_spec = jnp.mean(spec_real * spec_real + spec_imag * spec_imag) + 1e-06
    energy_ref = jnp.mean(ref_real * ref_real + ref_imag * ref_imag) + 1e-06
    freq_cols = jnp.arange(BAND, dtype=jnp.int32)
    freq_rows = freq_cols - BAND // 2
    offsets_y = center[0] + row_ids - total_rows // 2
    offsets_x = center[1] + jnp.arange(WIN_COLS, dtype=jnp.int32) - WIN_COLS // 2
    row_cos, row_sin = phase_pair(offsets_y, freq_rows, Y)
    col_cos, col_sin = phase_pair(freq_cols, offsets_x, X)
    half_real = matmul(row_cos, cross_real) - matmul(row_sin, cross_imag)
    half_imag = matmul(row_cos, cross_imag) + matmul(row_sin, cross_real)
    return (matmul(half_real, col_cos) - matmul(half_imag, col_sin)) / (
        BAND * jnp.sqrt(energy_spec * energy_ref)
    )


def per_device(
    volume,
    plane_shift,
    plane_weight,
    column_left,
    column_weight,
    window_center,
    tilt_owner,
    reference_band,
):
    devices = lax.axis_size("slab")
    position = lax.axis_index("slab")
    partials = []
    for which in range(TILTS):

        def rows_term(first_row, row_count, which=which):
            return reproject(
                volume,
                plane_shift[which],
                plane_weight[which],
                column_left[which],
                column_weight[which],
                row_count,
            )

        partials.append(band_part(rows_term(0, Y)))
    stacked = jnp.stack(partials)
    mine = reference_band[0]
    spectra = lax.psum(stacked, "slab")
    references = jnp.stack([from_root(mine, "slab", tilt_owner[which]) for which in range(TILTS)])
    total_rows = WIN_ROWS_DEV * devices
    outputs = []
    maxima = []
    row_ids = position * WIN_ROWS_DEV + jnp.arange(WIN_ROWS_DEV, dtype=jnp.int32)
    for which in range(TILTS):
        corr = correlate(
            spectra[which], references[which], window_center[which], row_ids, total_rows
        )
        outputs.append(corr)
        maxima.append(jnp.max(corr))
    peaks = lax.pmax(jnp.stack(maxima), "slab")
    return (jnp.stack(outputs), peaks)


def solution(mesh):
    placed = (
        P(("grp", "slab"), None, None),
        P("grp", "slab"),
        P("grp", "slab"),
        P("grp", None),
        P("grp", None),
        P("grp", None),
        P("grp"),
        P(("grp", "slab"), None, None, None),
    )
    return jax.shard_map(
        per_device,
        mesh=mesh,
        in_specs=placed,
        out_specs=(P("grp", "slab", None), P("grp")),
        check_vma=False,
    )
```

profile of v0, /device:TPU:0, one launch (start us, length us, event | category | flops | bytes accessed | tf_op | source)
XLA Modules:
  0.0 311.6 jit_solution(11527147601551082680)
XLA Ops:
  24.0 6.2 %copy.10 = bf16[2,1024,1024]{1,2,0:T(8,128)(2,1)} copy(bf16[2,1024,1024]{2,1,0:T(8,128)(2,1)} %param.10) | data formatting | bytes 8388608 | tf_op args[0]
  30.2 5.0 %pad_slice_fusion.1 = (bf16[1,1024,1154]{1,2,0:T(8,128)(2,1)S(1)}, bf16[1,1024,1154]{1,2,0:T(8,128)(2,1)}) fusion(bf16[2,1024,1024]{1,2,0:T(8,128)(2,1)} %copy.10), kind=kLoop, calls=%fused_computation.5 | loop fusion | bytes 8921088 | tf_op jit(solution)/shard_map/slice | solution.py:38
  35.2 12.6 %add_bitcast_fusion.1 = (f32[1024,1024]{0,1:T(8,128)}, f32[1024,1024]{0,1:T(8,128)}) fusion(bf16[1,1024,1154]{1,2,0:T(8,128)(2,1)} %get-tuple-element.11, s32[]{:T(128)S(6)} %select_n.127, f32[]{:T(128)} %bitcast.11, s32[]{:T(128)S(6)} %select_n.126, f32[]{:T(128)S(6)} %sub.140, bf16[1,1024,1154]{1,2,0:T(8,128)(2,1)S(1)} %get-tuple-element.10, ...), kind=kLoop, calls=%fused_computation.13 | loop fusion | flops 23068672 | bytes 25165888 | tf_op jit(solution)/shard_map/add | solution.py:45
  47.8 8.6 %gather_fusion.2 = f32[1024,1024]{1,0:T(8,128)} fusion(f32[1024,1024]{0,1:T(8,128)} %get-tuple-element.9, s32[1024]{0:T(1024)S(1)} %get-tuple-element.34), kind=kCustom, calls=%fused_computation.2.clone | custom fusion | bytes 8392704 | tf_op jit(solution)/shard_map/jit(_take)/gather | solution.py:46
  56.4 8.6 %gather_fusion.3 = f32[1024,1024]{1,0:T(8,128)} fusion(f32[1024,1024]{0,1:T(8,128)} %get-tuple-element.9, s32[1024]{0:T(1024)S(1)} %get-tuple-element.35), kind=kCustom, calls=%fused_computation.3.clone | custom fusion | bytes 8392704 | tf_op jit(solution)/shard_map/jit(_take)/gather | solution.py:47
  65.0 4.4 %fusion = f32[1024,1024]{0,1:T(8,128)S(1)} fusion(f32[1024,1024]{1,0:T(8,128)} %gather_fusion.3, f32[1024,1024]{1,0:T(8,128)} %gather_fusion.2, f32[1024]{0:T(1024)S(1)} %bitcast.250, f32[1024]{0:T(1024)S(1)} %bitcast.249, pred[1024]{0:T(1024)(128)(4,1)S(1)} %get-tuple-element.33, pred[1024]{0:T(1024)(128)(4,1)S(1)} %get-tuple-element.32), kind=kLoop, calls=%fused_computation.7 | loop fusion | flops 5242880 | bytes 12593152 | tf_op jit(solution)/shard_map/add | solution.py:48
  69.4 8.5 %fusion.32 = f32[1024,128]{1,0:T(8,128)S(1)} fusion(f32[1024,1024]{0,1:T(8,128)S(1)} %fusion), kind=kOutput, calls=%fused_computation.69 | convolution fusion | flops 1612447744 | bytes 4718592 | tf_op jit(solution)/shard_map/dot_general | solution.py:27
  77.9 21.3 %convolution_negate_fusion = f32[1024,128]{1,0:T(8,128)S(1)} fusion(f32[1024,1024]{0,1:T(8,128)S(1)} %fusion), kind=kOutput, calls=%fused_computation.14 | convolution fusion | flops 1612578816 | bytes 4718592 | tf_op jit(solution)/shard_map/dot_general | solution.py:27
  99.2 8.6 %gather_fusion = f32[1024,1024]{1,0:T(8,128)} fusion(f32[1024,1024]{0,1:T(8,128)} %get-tuple-element.8, s32[1024]{0:T(1024)S(1)} %get-tuple-element.30), kind=kCustom, calls=%fused_computation.clone | custom fusion | bytes 8392704 | tf_op jit(solution)/shard_map/jit(_take)/gather | solution.py:46
  107.8 8.6 %gather_fusion.1 = f32[1024,1024]{1,0:T(8,128)} fusion(f32[1024,1024]{0,1:T(8,128)} %get-tuple-element.8, s32[1024]{0:T(1024)S(1)} %get-tuple-element.31), kind=kCustom, calls=%fused_computation.1.clone | custom fusion | bytes 8392704 | tf_op jit(solution)/shard_map/jit(_take)/gather | solution.py:47
  116.4 4.0 %fusion.1 = f32[1024,1024]{0,1:T(8,128)S(1)} fusion(f32[1024,1024]{1,0:T(8,128)} %gather_fusion.1, f32[1024,1024]{1,0:T(8,128)} %gather_fusion, f32[1024]{0:T(1024)S(1)} %bitcast.248, f32[1024]{0:T(1024)S(1)} %bitcast.247, pred[1024]{0:T(1024)(128)(4,1)S(1)} %get-tuple-element.29, pred[1024]{0:T(1024)(128)(4,1)S(1)} %get-tuple-element.28), kind=kLoop, calls=%fused_computation.10 | loop fusion | flops 5242880 | bytes 12593152 | tf_op jit(solution)/shard_map/add | solution.py:48
  120.4 8.5 %fusion.34 = f32[1024,128]{1,0:T(8,128)S(1)} fusion(f32[1024,1024]{0,1:T(8,128)S(1)} %fusion.1), kind=kOutput, calls=%fused_computation.70 | convolution fusion | flops 1612447744 | bytes 4718592 | tf_op jit(solution)/shard_map/dot_general | solution.py:27
  128.9 8.9 %convolution_negate_fusion.1 = f32[1024,128]{1,0:T(8,128)S(1)} fusion(f32[1024,1024]{0,1:T(8,128)S(1)} %fusion.1), kind=kOutput, calls=%fused_computation.15 | convolution fusion | flops 1612578816 | bytes 4718592 | tf_op jit(solution)/shard_map/dot_general | solution.py:27
  137.9 3.0 fusion.42
  140.9 3.0 fusion.40
  143.9 3.0 fusion.3
  146.9 3.0 fusion.2
  149.9 3.0 fusion.46
  152.9 3.2 %fusion.44 = f32[128,128]{1,0:T(8,128)S(1)} fusion(f32[1024,128]{1,0:T(8,128)S(1)} %convolution_negate_fusion.1, s32[128]{0:T(128)S(1)} %iota_add_fusion), kind=kOutput, calls=%fused_computation.75 | convolution fusion | flops 203161600 | bytes 590336 | tf_op jit(solution)/shard_map/dot_general | solution.py:27
  156.1 3.0 fusion.5
  159.1 3.0 fusion.4
  168.7 91.1 %all-reduce.4.cloned.1.call-done = (f32[2,2,128,128]{3,2,1,0:T(8,128)}, f32[2,128,128]{2,1,0:T(8,128)}, f32[2,128,128]{2,1,0:T(8,128)}) async-done(((f32[2,2,128,128]{3,2,1,0:T(8,128)}, f32[2,128,128]{2,1,0:T(8,128)}, f32[2,128,128]{2,1,0:T(8,128)}), (f32[2,2,128,128]{3,2,1,0:T(8,128)}, f32[2,128,128]{2,1,0:T(8,128)}, f32[2,128,128]{2,1,0:T(8,128)})) %all-reduce.4.cloned.1.call-update) | async-done | bytes 524304 | tf_op jit(solution)/shard_map/psum | solution.py:113
  259.8 1.7 multiply_subtract_fusion.1
  271.8 32.3 %pmax.7 = f32[2]{0:T(128)} all-reduce(f32[2]{0:T(128)S(1)} %pad_maximum_fusion.2), channel_id=1, replica_groups=mesh['grp'=2,'slab'=16] {'slab'}, use_global_device_ids=true, to_apply=%region_9.11 | all-reduce | flops 2 | bytes 16 | tf_op jit(solution)/shard_map/pmax | solution.py:125
  (41 shorter events, 15.9 us)
Async XLA Ops:
  7.2 252.6 %all-reduce.4.cloned.1.call-start = ((), (), s32[]{:S(2)}) async-start(), calls=%async_computation | async-start | bytes 1048576 | tf_op jit(solution)/shard_map/psum | solution.py:113
  56.4 8.6 %copy-start.1 = (f32[2,1024]{1,0:T(2,128)S(1)}, f32[2,1024]{1,0:T(2,128)}, u32[]{:S(2)}) copy-start(f32[2,1024]{1,0:T(2,128)} %param.14) | copy-start | bytes 24580
  149.9 12.2 %copy-start.3 = (s32[16]{0:T(128)S(1)}, s32[16]{0:T(128)}, u32[]{:S(2)}) copy-start(s32[16]{0:T(128)} %param.16) | copy-start | bytes 196
  152.9 11.8 %copy-start = (f32[1,2,128,128]{3,2,1,0:T(8,128)S(1)}, f32[1,2,128,128]{3,2,1,0:T(8,128)}, u32[]{:S(2)}) copy-start(f32[1,2,128,128]{3,2,1,0:T(8,128)} %param.17) | copy-start | bytes 393220
  152.9 12.6 %copy-start.2 = (s32[2,2]{1,0:T(2,128)S(1)}, s32[2,2]{1,0:T(2,128)}, u32[]{:S(2)}) copy-start(s32[2,2]{1,0:T(2,128)} %param.15) | copy-start | bytes 52
Sparse Core Ops, SparseCore 0:
  165.6 94.1 all-reduce.3
where the time goes:
time: 318 us; the launch traced here: 312 us
  waiting for transfers between devices  91.1 us (29%)
  matrix products  75.9 us (24%)
  local copies, waits for them, and re-layouts  50.6 us (16%)
  between operations  32.7 us (10%)
  blocking collectives  32.3 us (10%)
  other arithmetic  29 us (9%)
    psum x1, waiting for transfers between devices, per_device(): spectra = lax.psum(stacked, 'slab')  91.1 us
    dot_general x24, matrix products, matmul(): jnp.dot(first, second, precision=lax.Precision.HIGHEST, preferred_element...  75.9 us
    pmax x1, blocking collectives, per_device(): peaks = lax.pmax(jnp.stack(maxima), 'slab')  32.3 us
    gather x2, local copies, waits for them, and re-layouts, reproject(): right_values = jnp.take(summed, left_cols + 1, axis=1)  17.2 us
    gather x2, local copies, waits for them, and re-layouts, reproject(): left_values = jnp.take(summed, left_cols, axis=1)  17.2 us
    add x1, other arithmetic, reproject(): summed + (1.0 - weights[plane_no]) * near_cells  12.6 us
    add x2, other arithmetic, reproject(): return (1.0 - right_share) * left_values + right_share * right_values  8.41 us
  transfers between devices with their start and end apart: 1, of which 1 were waited for; matrix products, arithmetic and copies ran while one was open for 1% of the time, Pallas kernels for 0%

commit v1 on v0

--- a/solution.py
+++ b/solution.py
@@ -110,7 +110,9 @@
         partials.append(band_part(rows_term(0, Y)))
     stacked = jnp.stack(partials)
     mine = reference_band[0]
-    spectra = lax.psum(stacked, "slab")
+    spectra = stacked
+    for hop in (1, 2, 4, 8):
+        spectra = spectra + lax.ppermute(spectra, "slab", [(dev, dev ^ hop) for dev in range(16)])
     references = jnp.stack([from_root(mine, "slab", tilt_owner[which]) for which in range(TILTS)])
     total_rows = WIN_ROWS_DEV * devices
     outputs = []

time: 318 us -> 329 us (1.035)
  starting transfers between devices: 0.04 us -> 8.05 us
  waiting for transfers between devices: 91.1 us -> 95.9 us
    ppermute x0 -> x4, waiting for transfers between devices: none -> 19.6 us  [per_device(): lax.ppermute(spectra, 'slab', [(dev, dev ^ hop) for dev in range(16)])]
    psum x1, waiting for transfers between devices: 91.1 us -> 76.3 us  [from_root(): return lax.psum(kept, axis)]
    ppermute x0 -> x4, starting transfers between devices: none -> 8.01 us  [per_device(): lax.ppermute(spectra, 'slab', [(dev, dev ^ hop) for dev in range(16)])]
  transfers between devices with their start and end apart: 1 -> 5, of which waited for: 1 -> 5; matrix products, arithmetic and copies ran while one was open for 1% -> 1% of each run, Pallas kernels for 0% -> 0%
where the time goes in v1:
time: 329 us; the launch traced here: 324 us
  waiting for transfers between devices  95.9 us (29%)
  matrix products  75.9 us (23%)
  local copies, waits for them, and re-layouts  50.5 us (15%)
  between operations  32.5 us (10%)
  blocking collectives  32.4 us (10%)
  other arithmetic  28.3 us (9%)
  starting transfers between devices  8.05 us (2%)
    psum x1, waiting for transfers between devices, from_root(): return lax.psum(kept, axis)  76.3 us
    dot_general x24, matrix products, matmul(): jnp.dot(first, second, precision=lax.Precision.HIGHEST, preferred_element...  75.9 us
    pmax x1, blocking collectives, per_device(): peaks = lax.pmax(jnp.stack(maxima), 'slab')  32.4 us
    ppermute x4, waiting for transfers between devices, per_device(): lax.ppermute(spectra, 'slab', [(dev, dev ^ hop) for dev in range(16)])  19.6 us
    gather x2, local copies, waits for them, and re-layouts, reproject(): right_values = jnp.take(summed, left_cols + 1, axis=1)  17.2 us
    gather x2, local copies, waits for them, and re-layouts, reproject(): left_values = jnp.take(summed, left_cols, axis=1)  17.2 us
    add x1, other arithmetic, reproject(): summed + (1.0 - weights[plane_no]) * near_cells  12.7 us
    add x2, other arithmetic, reproject(): return (1.0 - right_share) * left_values + right_share * right_values  8.41 us
  transfers between devices with their start and end apart: 5, of which 5 were waited for; matrix products, arithmetic and copies ran while one was open for 1% of the time, Pallas kernels for 0%

profile of v1, /device:TPU:0, one launch (start us, length us, event | category | flops | bytes accessed | tf_op | source)
XLA Modules:
  0.0 323.6 jit_solution(12975801401625733191)
XLA Ops:
  23.8 6.2 %copy.10 = bf16[2,1024,1024]{1,2,0:T(8,128)(2,1)} copy(bf16[2,1024,1024]{2,1,0:T(8,128)(2,1)} %param.10) | data formatting | bytes 8388608 | tf_op args[0]
  30.0 5.0 %pad_slice_fusion.1 = (bf16[1,1024,1154]{1,2,0:T(8,128)(2,1)S(1)}, bf16[1,1024,1154]{1,2,0:T(8,128)(2,1)}) fusion(bf16[2,1024,1024]{1,2,0:T(8,128)(2,1)} %copy.10), kind=kLoop, calls=%fused_computation.5 | loop fusion | bytes 8921088 | tf_op jit(solution)/shard_map/slice | solution.py:38
  35.0 12.7 %add_bitcast_fusion.1 = (f32[1024,1024]{0,1:T(8,128)}, f32[1024,1024]{0,1:T(8,128)}) fusion(bf16[1,1024,1154]{1,2,0:T(8,128)(2,1)} %get-tuple-element.10, s32[]{:T(128)S(6)} %select_n.127, f32[]{:T(128)} %bitcast.11, s32[]{:T(128)S(6)} %select_n.126, f32[]{:T(128)S(6)} %sub.140, bf16[1,1024,1154]{1,2,0:T(8,128)(2,1)S(1)} %get-tuple-element.9, ...), kind=kLoop, calls=%fused_computation.13 | loop fusion | flops 23068672 | bytes 25165888 | tf_op jit(solution)/shard_map/add | solution.py:45
  47.7 8.6 %gather_fusion.2 = f32[1024,1024]{1,0:T(8,128)} fusion(f32[1024,1024]{0,1:T(8,128)} %get-tuple-element.8, s32[1024]{0:T(1024)S(1)} %get-tuple-element.33), kind=kCustom, calls=%fused_computation.2.clone | custom fusion | bytes 8392704 | tf_op jit(solution)/shard_map/jit(_take)/gather | solution.py:46
  56.3 8.6 %gather_fusion.3 = f32[1024,1024]{1,0:T(8,128)} fusion(f32[1024,1024]{0,1:T(8,128)} %get-tuple-element.8, s32[1024]{0:T(1024)S(1)} %get-tuple-element.34), kind=kCustom, calls=%fused_computation.3.clone | custom fusion | bytes 8392704 | tf_op jit(solution)/shard_map/jit(_take)/gather | solution.py:47
  64.9 4.4 %fusion = f32[1024,1024]{0,1:T(8,128)S(1)} fusion(f32[1024,1024]{1,0:T(8,128)} %gather_fusion.3, f32[1024,1024]{1,0:T(8,128)} %gather_fusion.2, f32[1024]{0:T(1024)S(1)} %bitcast.250, f32[1024]{0:T(1024)S(1)} %bitcast.249, pred[1024]{0:T(1024)(128)(4,1)S(1)} %get-tuple-element.32, pred[1024]{0:T(1024)(128)(4,1)S(1)} %get-tuple-element.31), kind=kLoop, calls=%fused_computation.7 | loop fusion | flops 5242880 | bytes 12593152 | tf_op jit(solution)/shard_map/add | solution.py:48
  69.3 8.5 %fusion.32 = f32[1024,128]{1,0:T(8,128)S(1)} fusion(f32[1024,1024]{0,1:T(8,128)S(1)} %fusion), kind=kOutput, calls=%fused_computation.69 | convolution fusion | flops 1612447744 | bytes 4718592 | tf_op jit(solution)/shard_map/dot_general | solution.py:27
  77.8 21.3 %convolution_negate_fusion = f32[1024,128]{1,0:T(8,128)S(1)} fusion(f32[1024,1024]{0,1:T(8,128)S(1)} %fusion), kind=kOutput, calls=%fused_computation.14 | convolution fusion | flops 1612578816 | bytes 4718592 | tf_op jit(solution)/shard_map/dot_general | solution.py:27
  99.2 8.6 %gather_fusion = f32[1024,1024]{1,0:T(8,128)} fusion(f32[1024,1024]{0,1:T(8,128)} %get-tuple-element.7, s32[1024]{0:T(1024)S(1)} %get-tuple-element.29), kind=kCustom, calls=%fused_computation.clone | custom fusion | bytes 8392704 | tf_op jit(solution)/shard_map/jit(_take)/gather | solution.py:46
  107.8 8.6 %gather_fusion.1 = f32[1024,1024]{1,0:T(8,128)} fusion(f32[1024,1024]{0,1:T(8,128)} %get-tuple-element.7, s32[1024]{0:T(1024)S(1)} %get-tuple-element.30), kind=kCustom, calls=%fused_computation.1.clone | custom fusion | bytes 8392704 | tf_op jit(solution)/shard_map/jit(_take)/gather | solution.py:47
  116.4 4.0 %fusion.1 = f32[1024,1024]{0,1:T(8,128)S(1)} fusion(f32[1024,1024]{1,0:T(8,128)} %gather_fusion.1, f32[1024,1024]{1,0:T(8,128)} %gather_fusion, f32[1024]{0:T(1024)S(1)} %bitcast.248, f32[1024]{0:T(1024)S(1)} %bitcast.247, pred[1024]{0:T(1024)(128)(4,1)S(1)} %get-tuple-element.28, pred[1024]{0:T(1024)(128)(4,1)S(1)} %get-tuple-element.27), kind=kLoop, calls=%fused_computation.10 | loop fusion | flops 5242880 | bytes 12593152 | tf_op jit(solution)/shard_map/add | solution.py:48
  120.4 8.5 %fusion.34 = f32[1024,128]{1,0:T(8,128)S(1)} fusion(f32[1024,1024]{0,1:T(8,128)S(1)} %fusion.1), kind=kOutput, calls=%fused_computation.70 | convolution fusion | flops 1612447744 | bytes 4718592 | tf_op jit(solution)/shard_map/dot_general | solution.py:27
  128.9 8.9 %convolution_negate_fusion.1 = f32[1024,128]{1,0:T(8,128)S(1)} fusion(f32[1024,1024]{0,1:T(8,128)S(1)} %fusion.1), kind=kOutput, calls=%fused_computation.15 | convolution fusion | flops 1612578816 | bytes 4718592 | tf_op jit(solution)/shard_map/dot_general | solution.py:27
  143.8 3.0 fusion.3
  146.8 3.0 fusion.2
  149.8 3.0 fusion.46
  152.8 3.2 fusion.44
  156.0 3.0 fusion.5
  159.1 3.0 fusion.4
  166.8 6.6 %collective-permute-done.1 = f32[2,2,128,128]{3,2,1,0:T(8,128)S(1)} collective-permute-done((f32[2,2,128,128]{3,2,1,0:T(8,128)S(1)}, f32[2,2,128,128]{3,2,1,0:T(8,128)S(1)}, u32[]{:S(2)}, u32[]{:S(2)}) %collective-permute-start.1) | collective-permute-done | bytes 262176 | tf_op jit(solution)/shard_map/ppermute | solution.py:115
  177.9 3.4 %collective-permute-done.2 = f32[2,2,128,128]{3,2,1,0:T(8,128)S(1)} collective-permute-done((f32[2,2,128,128]{3,2,1,0:T(8,128)S(1)}, f32[2,2,128,128]{3,2,1,0:T(8,128)S(1)}, u32[]{:S(2)}, u32[]{:S(2)}) %collective-permute-start.2) | collective-permute-done | bytes 262176 | tf_op jit(solution)/shard_map/ppermute | solution.py:115
  187.1 8.4 %collective-permute-done.3 = f32[2,2,128,128]{3,2,1,0:T(8,128)S(1)} collective-permute-done((f32[2,2,128,128]{3,2,1,0:T(8,128)S(1)}, f32[2,2,128,128]{3,2,1,0:T(8,128)S(1)}, u32[]{:S(2)}, u32[]{:S(2)}) %collective-permute-start.3) | collective-permute-done | bytes 262176 | tf_op jit(solution)/shard_map/ppermute | solution.py:115
  195.6 76.3 %all-reduce.4.cloned.1.call-done = (f32[2,128,128]{2,1,0:T(8,128)}, f32[2,128,128]{2,1,0:T(8,128)}) async-done(((f32[2,128,128]{2,1,0:T(8,128)}, f32[2,128,128]{2,1,0:T(8,128)}), (f32[2,128,128]{2,1,0:T(8,128)}, f32[2,128,128]{2,1,0:T(8,128)})) %all-reduce.4.cloned.1.call-update) | async-done | bytes 262160 | tf_op jit(solution)/shard_map/psum | solution.py:17
  283.6 32.4 %pmax.7 = f32[2]{0:T(128)} all-reduce(f32[2]{0:T(128)S(1)} %pad_maximum_fusion.2), channel_id=1, replica_groups=mesh['grp'=2,'slab'=16] {'slab'}, use_global_device_ids=true, to_apply=%region_8.10 | all-reduce | flops 2 | bytes 16 | tf_op jit(solution)/shard_map/pmax | solution.py:127
  (53 shorter events, 31.9 us)
Async XLA Ops:
  7.2 264.7 %all-reduce.4.cloned.1.call-start = ((), (), s32[]{:S(2)}) async-start(), calls=%async_computation | async-start | bytes 524288 | tf_op jit(solution)/shard_map/psum | solution.py:17
  56.3 8.6 %copy-start.1 = (f32[2,1024]{1,0:T(2,128)S(1)}, f32[2,1024]{1,0:T(2,128)}, u32[]{:S(2)}) copy-start(f32[2,1024]{1,0:T(2,128)} %param.14) | copy-start | bytes 24580
  156.0 19.4 %copy-start.3 = (s32[16]{0:T(128)S(1)}, s32[16]{0:T(128)}, u32[]{:S(2)}) copy-start(s32[16]{0:T(128)} %param.16) | copy-start | bytes 196
  156.0 21.1 %copy-start = (f32[1,2,128,128]{3,2,1,0:T(8,128)S(1)}, f32[1,2,128,128]{3,2,1,0:T(8,128)}, u32[]{:S(2)}) copy-start(f32[1,2,128,128]{3,2,1,0:T(8,128)} %param.17) | copy-start | bytes 393220
  156.0 27.9 %copy-start.2 = (s32[2,2]{1,0:T(2,128)S(1)}, s32[2,2]{1,0:T(2,128)}, u32[]{:S(2)}) copy-start(s32[2,2]{1,0:T(2,128)} %param.15) | copy-start | bytes 52
  162.1 1.7 collective-permute-start
  163.9 9.5 %collective-permute-start.1 = (f32[2,2,128,128]{3,2,1,0:T(8,128)S(1)}, f32[2,2,128,128]{3,2,1,0:T(8,128)S(1)}, u32[]{:S(2)}, u32[]{:S(2)}) collective-permute-start(f32[2,2,128,128]{3,2,1,0:T(8,128)S(1)} %fusion.198), channel_id=1, source_target_pairs={{0,2},{1,3},{2,0},{3,1},{4,6},{5,7},{6,4},{7,5},{8,10},{9,11},{10,... | collective-permute-start | bytes 786440 | tf_op jit(solution)/shard_map/ppermute | solution.py:115
  173.5 7.8 %collective-permute-start.2 = (f32[2,2,128,128]{3,2,1,0:T(8,128)S(1)}, f32[2,2,128,128]{3,2,1,0:T(8,128)S(1)}, u32[]{:S(2)}, u32[]{:S(2)}) collective-permute-start(f32[2,2,128,128]{3,2,1,0:T(8,128)S(1)} %fusion.238), channel_id=1, source_target_pairs={{0,4},{1,5},{2,6},{3,7},{4,0},{5,1},{6,2},{7,3},{8,12},{9,13},{10,... | collective-permute-start | bytes 786440 | tf_op jit(solution)/shard_map/ppermute | solution.py:115
  181.3 14.2 %collective-permute-start.3 = (f32[2,2,128,128]{3,2,1,0:T(8,128)S(1)}, f32[2,2,128,128]{3,2,1,0:T(8,128)S(1)}, u32[]{:S(2)}, u32[]{:S(2)}) collective-permute-start(f32[2,2,128,128]{3,2,1,0:T(8,128)S(1)} %add.327), channel_id=1, source_target_pairs={{0,8},{1,9},{2,10},{3,11},{4,12},{5,13},{6,14},{7,15},{8,0},{9,1},... | collective-permute-start | bytes 786440 | tf_op jit(solution)/shard_map/ppermute | solution.py:115
Sparse Core Ops, SparseCore 0:
  178.0 93.8 all-reduce.3
